TPU v7x, 256 devices: a whole 4x4x8 slice. The times are simulated.
256 devices in a mesh: patch: 64 (over y, z, core), sub: 4 (over x).
Axes of the slice: x: 4, y: 4, z: 8, core: 2. Of those that a mesh axis runs over, the one named last changes fastest.
Arguments:
- state: float32 [64, 4, 1, 27, 729], P('patch', 'sub'), may hold values from -6 to 6
- stiff_weight: float32 [64, 96, 9216], P('patch'), may hold values from 0.3 to 3
- volume_weight: float32 [64, 96, 9216], P('patch'), may hold values from 0.5 to 2
- lagrange: float32 [256, 4, 1, 729], P('patch', 'sub'), may hold values from -6 to 6
- mortar: float32 [256, 2, 2, 27, 27], P('patch'), may hold values from -1.25 to 1.25
- links: int32 [256, 6], replicated, may hold values from 0 to 63, as said below
Outputs:
- residual: float32 [64, 4, 1, 27, 729], P('patch', 'sub')
- constraint: float32 [256, 4, 1, 729], P('patch', 'sub')
Inputs may be any that keep to these rules, and one draw needn't show every extreme that they name: `links`: row o * 4 + s is slot s of owner o along patch. Live slots of an owner come first and have both counts in 12 to 27; empty slots are all zero. 2 * 64 slots are live. A live interface joins face 2d + 1 of its first patch to face 2d of its second patch, d being 0 or 1; faces 0 to 3 of every patch lie on exactly one live interface each; the live interfaces of one owner all have the same d. At most 2 faces of one patch lie on live interfaces of one owner; in every draw some owner has 4 live slots and 2 faces of one patch.
All inputs are finite; a program needn't handle non-finite values.
Results may differ from a plain program's by a relative error of at most 0.0001.
Values sent between devices are 32-bit elements; how exact they have to be, the bound alone decides.
A program may use at most 128 MiB of HBM per device.

v0:
```python
import jax
import jax.numpy as jnp
import numpy as np
from jax import lax
from jax.sharding import PartitionSpec as P

ELEMS = 24
DEGREE = 3
FIELDS = 4
stabilize = 0.25
highest = lax.Precision.HIGHEST
gauss_points_four = [
    -0.8611363115940526,
    -0.3399810435848563,
    0.3399810435848563,
    0.8611363115940526,
]
gauss_weights_four = [
    0.3478548451374538,
    0.6521451548625461,
    0.6521451548625461,
    0.3478548451374538,
]


def filled_up(lines, peers):
    spare = -lines.shape[0] % peers
    if not spare:
        return lines
    return jnp.concatenate([lines, jnp.zeros((spare, *lines.shape[1:]), lines.dtype)])


def spread(value, axis, root):
    lines = jnp.where(lax.axis_index(axis) == root, value, jnp.zeros_like(value)).reshape(
        -1, *value.shape[1:][-1:]
    )
    padded = filled_up(lines, lax.axis_size(axis))
    own = lax.psum_scatter(padded, axis, scatter_dimension=0, tiled=True)
    return lax.all_gather(own, axis, axis=0, tiled=True)[: len(lines)].reshape(value.shape)


def in_order(tiles, dim):
    dims = list(tiles.shape[1:])
    dims[dim] *= tiles.shape[0]
    return jnp.moveaxis(tiles, 0, dim).reshape(dims)


def from_everyone(value, axis):
    peers = lax.axis_size(axis)
    return lax.all_to_all(
        jnp.broadcast_to(value[None], (peers, *value.shape)), axis, 0, 0, tiled=True
    )


def gathered_copies(value, axis, dim):
    return in_order(from_everyone(value, axis), dim)


def spline_tables(elements, degree):
    knot_list = np.concatenate(
        [np.zeros(degree), np.arange(elements + 1.0), np.full(degree, float(elements))]
    )
    gauss_nodes = np.array(gauss_points_four)
    gauss_weights = np.array(gauss_weights_four)
    points = (np.arange(elements)[:, None] + (gauss_nodes[None, :] + 1.0) / 2.0).reshape(-1)
    point_weights = np.tile(gauss_weights / 2.0, elements)
    current = np.where(
        (knot_list[None, :-1] <= points[:, None]) & (points[:, None] < knot_list[None, 1:]),
        1.0,
        0.0,
    )
    previous = current
    for order_k in range(1, degree + 1):
        previous = current
        amount = len(knot_list) - 1 - order_k
        current = np.zeros((points.shape[0], amount))
        for column in range(amount):
            left_span = knot_list[column + order_k] - knot_list[column]
            right_span = knot_list[column + order_k + 1] - knot_list[column + 1]
            if left_span > 0:
                current[:, column] += (points - knot_list[column]) / left_span * previous[:, column]
            if right_span > 0:
                current[:, column] += (
                    (knot_list[column + order_k + 1] - points)
                    / right_span
                    * previous[:, column + 1]
                )
    slope_part = np.zeros(current.shape)
    for column in range(current.shape[1]):
        left_span = knot_list[column + degree] - knot_list[column]
        right_span = knot_list[column + degree + 1] - knot_list[column + 1]
        if left_span > 0:
            slope_part[:, column] += degree / left_span * previous[:, column]
        if right_span > 0:
            slope_part[:, column] -= degree / right_span * previous[:, column + 1]
    return (
        jnp.asarray(current, jnp.float32),
        jnp.asarray(slope_part, jnp.float32),
        jnp.asarray(current * point_weights[:, None], jnp.float32),
        jnp.asarray(slope_part * point_weights[:, None], jnp.float32),
    )


def forward(coefficients, outer_matrix, middle_matrix, inner_matrix):
    size_n = outer_matrix.shape[1]
    partial_value = coefficients.reshape(size_n, size_n, size_n)
    partial_value = jnp.einsum("ck,ijk->ijc", inner_matrix, partial_value, precision=highest)
    partial_value = jnp.einsum("bj,ijc->ibc", middle_matrix, partial_value, precision=highest)
    return jnp.dot(
        outer_matrix,
        partial_value.reshape(size_n, -1),
        precision=highest,
        preferred_element_type=jnp.float32,
    )


def backward(values, outer_matrix, middle_matrix, inner_matrix):
    size_n = outer_matrix.shape[1]
    points = outer_matrix.shape[0]
    partial_value = jnp.dot(
        outer_matrix.T, values, precision=highest, preferred_element_type=jnp.float32
    )
    partial_value = partial_value.reshape(size_n, points, points)
    partial_value = jnp.einsum("bj,ibc->ijc", middle_matrix, partial_value, precision=highest)
    partial_value = jnp.einsum("ck,ijc->ijk", inner_matrix, partial_value, precision=highest)
    return partial_value.reshape(size_n, size_n * size_n)


def gradients(coefficients, value_table, slope_table):
    size_n = value_table.shape[1]
    field_cube = coefficients.reshape(size_n, size_n, size_n)
    last_value = jnp.einsum("ck,ijk->ijc", value_table, field_cube, precision=highest)
    last_slope = jnp.einsum("ck,ijk->ijc", slope_table, field_cube, precision=highest)
    mid_plain = jnp.einsum("bj,ijc->ibc", value_table, last_value, precision=highest).reshape(
        size_n, -1
    )
    mid_second = jnp.einsum("bj,ijc->ibc", slope_table, last_value, precision=highest).reshape(
        size_n, -1
    )
    mid_third = jnp.einsum("bj,ijc->ibc", value_table, last_slope, precision=highest).reshape(
        size_n, -1
    )
    return (
        jnp.dot(slope_table, mid_plain, precision=highest, preferred_element_type=jnp.float32),
        jnp.dot(value_table, mid_second, precision=highest, preferred_element_type=jnp.float32),
        jnp.dot(value_table, mid_third, precision=highest, preferred_element_type=jnp.float32),
    )


def backward_sum(fluxes, value_weighted, slope_weighted):
    size_n = value_weighted.shape[1]
    points = value_weighted.shape[0]
    head_first = jnp.dot(slope_weighted.T, fluxes[0], precision=highest).reshape(
        size_n, points, points
    )
    head_second = jnp.dot(value_weighted.T, fluxes[1], precision=highest).reshape(
        size_n, points, points
    )
    head_third = jnp.dot(value_weighted.T, fluxes[2], precision=highest).reshape(
        size_n, points, points
    )
    plain_mid = jnp.einsum("bj,ibc->ijc", value_weighted, head_first, precision=highest)
    plain_mid = plain_mid + jnp.einsum(
        "bj,ibc->ijc", slope_weighted, head_second, precision=highest
    )
    third_mid = jnp.einsum("bj,ibc->ijc", value_weighted, head_third, precision=highest)
    result = jnp.einsum("ck,ijc->ijk", value_weighted, plain_mid, precision=highest)
    result = result + jnp.einsum("ck,ijc->ijk", slope_weighted, third_mid, precision=highest)
    return result.reshape(size_n, size_n * size_n)


def volume_terms(own_field, pressure, stiffness, volume, factor, picker, tables):
    value_table, slope_table, value_weighted, slope_weighted = tables
    partials = gradients(own_field, value_table, slope_table)
    pvalue = forward(pressure, value_table, value_table, value_table)
    fluxes = [factor * stiffness * partials[d] - picker[d] * volume * pvalue for d in range(3)]
    result = backward_sum(fluxes, value_weighted, slope_weighted)
    chosen = picker[0] * partials[0] + picker[1] * partials[1] + picker[2] * partials[2]
    return (result, -backward(volume * chosen, value_weighted, value_weighted, value_weighted))


def per_device(state, stiff_weight, volume_weight, lagrange, mortar, links):
    tables = spline_tables(ELEMS, DEGREE)
    patches = lax.axis_size("patch")
    device = lax.axis_index("patch")
    field_index = lax.axis_index("sub")
    vectors = state.shape[2]
    size_n = state.shape[3]
    slot_count = mortar.shape[0]
    coefficients = state[0, 0]
    stiffness = stiff_weight[0]
    volume = volume_weight[0]
    is_pressure = field_index == FIELDS - 1
    factor = jnp.where(is_pressure, -stabilize, 1.0).astype(jnp.float32)
    picker = (jnp.arange(3) == field_index).astype(jnp.float32)

    def terms_of():

        def one_vector(paired):
            return volume_terms(paired[0], paired[1], stiffness, volume, factor, picker, tables)

        return one_vector

    pressure = spread(coefficients, "sub", FIELDS - 1)
    own_terms, div_terms = lax.map(terms_of(), (coefficients, pressure))
    divergence = lax.psum(div_terms, "sub")
    residual = own_terms + jnp.where(is_pressure, divergence, 0.0)
    field_cube = coefficients.reshape(vectors, size_n, size_n, size_n)
    faces = jnp.stack(
        [field_cube[:, 0], field_cube[:, -1], field_cube[:, :, 0], field_cube[:, :, -1]]
    )
    faces = faces.reshape(4, vectors, size_n * size_n)
    item_count = 2 * slot_count
    item_patch = links[:, 0:2].reshape(patches, item_count)
    item_face = links[:, 2:4].reshape(patches, item_count)
    is_live = jnp.repeat(links[:, 4] > 0, 2).reshape(patches, item_count)
    own_patch = lax.dynamic_index_in_dim(item_patch, device, 0, keepdims=False)
    own_face = lax.dynamic_index_in_dim(item_face, device, 0, keepdims=False)
    own_live = lax.dynamic_index_in_dim(is_live, device, 0, keepdims=False)
    own_rows = lax.dynamic_slice_in_dim(links, device * slot_count, slot_count, 0)
    face_grid = jnp.arange(4)
    gathered = gathered_copies(faces[None], "patch", 0)
    picked = jnp.take(
        gathered.reshape(patches * 4, vectors, size_n * size_n), own_patch * 4 + own_face, axis=0
    )
    picked = picked * own_live.astype(jnp.float32)[:, None, None]
    rank_grid = jnp.arange(size_n)
    row_mask = (rank_grid[None, :] < own_rows[:, 4:5]).astype(jnp.float32)
    col_mask = (rank_grid[None, :] < own_rows[:, 5:6]).astype(jnp.float32)
    left = mortar[:, :, 0] * row_mask[:, None, :, None]
    right = mortar[:, :, 1] * col_mask[:, None, :, None]
    traces_here = picked.reshape(slot_count, 2, vectors, size_n, size_n)
    projected = jnp.einsum("sgai,sgvij,sgbj->sgvab", left, traces_here, right, precision=highest)
    constraint = (projected[:, 0] - projected[:, 1]).reshape(
        slot_count, 1, vectors, size_n * size_n
    )
    multipliers = lagrange[:, 0].reshape(slot_count, vectors, size_n, size_n)
    signs = jnp.array([1.0, -1.0], jnp.float32)
    correction = jnp.einsum("sgai,svab,sgbj->sgvij", left, multipliers, right, precision=highest)
    correction = (correction * signs[None, :, None, None, None]).reshape(
        item_count, vectors, size_n * size_n
    )
    all_blocks = lax.all_gather(correction, "patch", axis=0, tiled=True)
    face_match = (
        (is_live & (item_patch == device)).reshape(-1)[None, :]
        & (item_face.reshape(-1)[None, :] == face_grid[:, None])
    ).astype(jnp.float32)
    face_total = jnp.einsum("ft,tvx->fvx", face_match, all_blocks, precision=highest)
    pieces = face_total.reshape(4, vectors, size_n, size_n)
    result_cube = residual.reshape(vectors, size_n, size_n, size_n)
    result_cube = result_cube.at[:, 0].add(pieces[0])
    result_cube = result_cube.at[:, -1].add(pieces[1])
    result_cube = result_cube.at[:, :, 0].add(pieces[2])
    result_cube = result_cube.at[:, :, -1].add(pieces[3])
    return (result_cube.reshape(1, 1, vectors, size_n, size_n * size_n), constraint)


def solution(mesh):
    return jax.shard_map(
        per_device,
        mesh=mesh,
        in_specs=(
            P("patch", "sub", None, None, None),
            P("patch", None, None),
            P("patch", None, None),
            P("patch", "sub", None, None),
            P("patch", None, None, None, None),
            P(),
        ),
        out_specs=(P("patch", "sub", None, None, None), P("patch", "sub", None, None)),
        check_vma=False,
    )
```

profile of v0, /device:TPU:1, one launch (start us, length us, event | category | flops | bytes accessed | tf_op | source)
XLA Modules:
  0.0 175.8 jit_solution(12599876094862100393)
XLA Ops:
  8.9 10.5 %fusion = f32[8,729]{1,0:T(8,128)S(1)} fusion(f32[28,729]{1,0:T(8,128)S(1)} %concatenate.12), kind=kCustom, calls=%all-reduce-scatter | all-reduce-scatter fusion | flops 23329 | bytes 106000
  19.5 2.8 %collective-permute-start = (f32[3,729]{1,0:T(4,128)S(1)}, f32[3,729]{1,0:T(4,128)S(1)}, u32[]{:S(2)}, u32[]{:S(2)}) collective-permute-start(f32[3,729]{1,0:T(4,128)S(1)} %slice.223), channel_id=1, source_target_pairs={{0,1},{1,2},{2,3},{4,5},{5,6},{6,7},{8,9},{9,10},{10,11},{12,13},{... | collective-permute-start | bytes 26252
  25.3 15.1 %all-to-all-start = ((f32[64,1,4,1,729]{4,2,3,1,0:T(4,128)}), f32[64,1,4,1,729]{4,2,3,1,0:T(4,128)}, u32[]{:S(2)}, u32[]{:S(2)}) async-start(f32[64,1,4,1,729]{4,2,3,1,0:T(4,128)} %broadcast_in_dim.45), calls=%async_computation | async-start | bytes 1572864 | tf_op jit(solution)/shard_map/all_to_all | solution.py:50
  42.2 2.2 %convolution_bitcast_fusion.1 = f32[27,96,96]{1,2,0:T(8,128)S(1)} fusion(f32[27,27,96]{2,1,0:T(8,128)S(1)} %convolution_bitcast_fusion.7, f32[96,27,1]{0,1,2:T(8,128)S(1)} %copy-done.21), kind=kOutput, calls=%fused_computation.38 | convolution fusion | flops 80621568 | bytes 1285632 | tf_op jit(solution)/shard_map/while/body/eval_jaxpr/bj,ijc->ibc/dot_general | solution.py:137
  44.5 2.2 %convolution_bitcast_fusion.3 = f32[27,96,96]{1,2,0:T(8,128)S(1)} fusion(f32[27,27,96]{2,1,0:T(8,128)S(1)} %convolution_bitcast_fusion.7, f32[96,27,1]{0,1,2:T(8,128)S(1)} %copy-done.15), kind=kOutput, calls=%fused_computation.40 | convolution fusion | flops 80621568 | bytes 1285632 | tf_op jit(solution)/shard_map/while/body/eval_jaxpr/bj,ijc->ibc/dot_general | solution.py:134
  47.3 3.3 %convolution_bitcast_fusion = f32[27,96,96]{1,2,0:T(8,128)} fusion(f32[27,27,96]{2,1,0:T(8,128)S(1)} %convolution_bitcast_fusion.6, f32[96,27,1]{0,1,2:T(8,128)S(1)} %copy-done.15), kind=kOutput, calls=%fused_computation.37 | convolution fusion | flops 80621568 | bytes 1285632 | tf_op jit(solution)/shard_map/while/body/eval_jaxpr/bj,ijc->ibc/dot_general | solution.py:140
  50.6 2.8 %copy.46 = f32[27,96,96]{2,1,0:T(8,128)} copy(f32[27,96,96]{1,2,0:T(8,128)} %convolution_bitcast_fusion) | data formatting | bytes 1990656 | tf_op jit(solution)/shard_map/while/body/eval_jaxpr/bj,ijc->ibc/transpose | solution.py:140
  53.5 3.1 %reshape.439 = f32[27,9216]{1,0:T(8,128)} reshape(f32[27,96,96]{2,1,0:T(8,128)} %copy.46) | data formatting | bytes 1990656 | tf_op jit(solution)/shard_map/while/body/eval_jaxpr/reshape | solution.py:140
  58.1 3.2 %reshape.437 = f32[27,9216]{1,0:T(8,128)} reshape(f32[27,96,96]{2,1,0:T(8,128)} %copy.45) | data formatting | bytes 1990656 | tf_op jit(solution)/shard_map/while/body/eval_jaxpr/reshape | solution.py:137
  63.6 4.7 %fusion.68 = f32[96,9216]{1,0:T(8,128)S(1)} fusion(f32[96,27]{0,1:T(8,128)S(1)} %copy-done.17, f32[27,9216]{1,0:T(8,128)} %reshape.437), kind=kOutput, calls=%fused_computation.118 | convolution fusion | flops 286654464 | bytes 4544640 | tf_op jit(solution)/shard_map/while/body/eval_jaxpr/dot_general | solution.py:145
  68.3 3.0 %fusion.70 = f32[96,9216]{1,0:T(8,128)S(1)} fusion(f32[96,27]{0,1:T(8,128)S(1)} %copy-done.17, f32[27,9216]{1,0:T(8,128)S(1)} %copy-done.8), kind=kOutput, calls=%fused_computation.120 | convolution fusion | flops 286654464 | bytes 4544640 | tf_op jit(solution)/shard_map/while/body/eval_jaxpr/dot_general | solution.py:146
  71.4 3.0 %fusion.64 = f32[96,9216]{1,0:T(8,128)S(1)} fusion(f32[96,27]{0,1:T(8,128)S(1)} %copy-done.23, f32[27,9216]{1,0:T(8,128)S(1)} %copy-done.9), kind=kOutput, calls=%fused_computation.114 | convolution fusion | flops 286654464 | bytes 4544640 | tf_op jit(solution)/shard_map/while/body/eval_jaxpr/dot_general | solution.py:144
  76.2 4.4 %fusion.13 = f32[27,9216]{1,0:T(8,128)S(1)} fusion(f32[96,27]{0,1:T(8,128)S(1)} %copy-done.18, f32[1,96,9216]{2,1,0:T(8,128)S(1)} %copy-done, f32[96,9216]{1,0:T(8,128)S(1)} %fusion.70, f32[96,9216]{1,0:T(8,128)S(1)} %fusion.68, f32[96,9216]{1,0:T(8,128)S(1)} %fusion.64, f32[]{:T(128)} %bitcast.17, f32[]{:T(128)} %bitcast.12, f32[]{:T(128)} %bitcast.4), kind=kOutput, calls=%fused_computation.14 | convolution fusion | flops 291962880 | bytes 15161484 | tf_op jit(solution)/shard_map/while/body/eval_jaxpr/dot_general | solution.py:120
  93.5 9.1 %all-gather = f32[4,7,729]{2,1,0:T(8,128)S(1)} all-gather(f32[1,7,729]{2,1,0:T(8,128)S(1)} %dynamic-slice_bitcast_fusion), channel_id=1, replica_groups=mesh['patch'=64,'sub'=4] {'sub'}, dimensions={0}, use_global_device_ids=true | all-gather | bytes 102060 | tf_op jit(solution)/shard_map/all_gather | solution.py:39
  103.6 2.2 %convolution_bitcast_fusion.2 = f32[27,96,96]{1,2,0:T(8,128)S(1)} fusion(f32[27,27,96]{2,1,0:T(8,128)S(1)} %fusion.65, f32[96,27,1]{0,1,2:T(8,128)S(1)} %copy-done.15), kind=kOutput, calls=%fused_computation.39 | convolution fusion | flops 80621568 | bytes 1285632 | tf_op jit(solution)/shard_map/while/body/eval_jaxpr/bj,ijc->ibc/dot_general | solution.py:108
  108.2 4.4 %fusion.66 = f32[96,9216]{1,0:T(8,128)S(1)} fusion(f32[96,27]{0,1:T(8,128)} %constant.177.clone, f32[27,9216]{1,0:T(8,128)} %reshape.435), kind=kOutput, calls=%fused_computation.116 | convolution fusion | flops 286654464 | bytes 4544640 | tf_op jit(solution)/shard_map/while/body/eval_jaxpr/dot_general | solution.py:109
  112.7 7.8 %fusion.7 = f32[27,9216]{1,0:T(8,128)} fusion(f32[96,27]{0,1:T(8,128)S(1)} %copy-done.19, f32[96,9216]{1,0:T(8,128)S(1)} %fusion.66, f32[1,96,9216]{2,1,0:T(8,128)S(1)} %copy-done.1, f32[96,9216]{1,0:T(8,128)} %copy-done.4, f32[1,96,9216]{2,1,0:T(8,128)} %param.20, f32[]{:T(128)} %bitcast.12, f32[]{:T(128)S(6)} %select_n.60), kind=kOutput, calls=%fused_computation.10 | convolution fusion | flops 291078144 | bytes 15161480 | tf_op jit(solution)/shard_map/while/body/eval_jaxpr/dot_general | solution.py:156
  120.5 4.1 %fusion.3 = f32[27,9216]{1,0:T(8,128)} fusion(f32[96,27]{0,1:T(8,128)S(1)} %copy-done.22, f32[96,9216]{1,0:T(8,128)S(1)} %fusion.66, f32[1,96,9216]{2,1,0:T(8,128)S(1)} %copy-done.1, f32[96,9216]{1,0:T(8,128)S(1)} %copy-done.6, f32[1,96,9216]{2,1,0:T(8,128)S(1)} %copy-done.2, f32[]{:T(128)} %bitcast.4, f32[]{:T(128)S(6)} %select_n.60), kind=kOutput, calls=%fused_computation.7 | convolution fusion | flops 291078144 | bytes 15161480 | tf_op jit(solution)/shard_map/while/body/eval_jaxpr/dot_general | solution.py:153
  124.6 3.1 %reshape.436 = f32[27,96,96]{2,1,0:T(8,128)} reshape(f32[27,9216]{1,0:T(8,128)} %fusion.3) | data formatting | bytes 1990656 | tf_op jit(solution)/shard_map/while/body/eval_jaxpr/reshape | solution.py:153
  127.7 2.9 %reshape.438 = f32[27,96,96]{2,1,0:T(8,128)} reshape(f32[27,9216]{1,0:T(8,128)} %fusion.7) | data formatting | bytes 1990656 | tf_op jit(solution)/shard_map/while/body/eval_jaxpr/reshape | solution.py:156
  130.6 8.2 %fusion.11 = f32[27,9216]{1,0:T(8,128)} fusion(f32[96,27]{0,1:T(8,128)} %constant.179.clone, f32[96,9216]{1,0:T(8,128)S(1)} %fusion.66, f32[1,96,9216]{2,1,0:T(8,128)} %param.21, f32[96,9216]{1,0:T(8,128)} %copy-done.3, f32[1,96,9216]{2,1,0:T(8,128)} %param.20, f32[]{:T(128)} %bitcast.17, f32[]{:T(128)S(6)} %select_n.60), kind=kOutput, calls=%fused_computation.13 | convolution fusion | flops 291078144 | bytes 15161480 | tf_op jit(solution)/shard_map/while/body/eval_jaxpr/dot_general | solution.py:159
  140.7 2.2 %fusion.67 = f32[27,96,27]{1,2,0:T(8,128)S(1)} fusion(f32[27,96,96]{2,1,0:T(8,128)} %reshape.436, f32[96,27,1]{0,1,2:T(8,128)S(1)} %copy-done.14), kind=kOutput, calls=%fused_computation.117 | convolution fusion | flops 80621568 | bytes 1285632 | tf_op jit(solution)/shard_map/while/body/eval_jaxpr/bj,ibc->ijc/dot_general | solution.py:162
  150.2 14.0 %all-gather.3.cloned.1.call-done = f32[512,1,729]{2,0,1:T(8,128)} async-done(((f32[8,1,729]{2,0,1:T(8,128)}), f32[512,1,729]{2,0,1:T(8,128)}) %all-gather.3.cloned.1.call-update) | async-done | bytes 1493008 | tf_op jit(solution)/shard_map/all_gather | solution.py:243
  164.3 2.0 %fusion.31 = f32[4,729]{1,0:T(4,128)S(1)} fusion(f32[512,1,729]{2,0,1:T(8,128)} %all-gather.3.cloned.1.call-done, s32[512]{0:T(512)S(1)} %copy-done.26, pred[512]{0:T(512)(128)(4,1)S(1)} %copy-done.28), kind=kOutput, calls=%fused_computation.35 | convolution fusion | flops 17920000 | bytes 1507216 | tf_op jit(solution)/shard_map/ft,tvx->fvx/dot_general | solution.py:248
  (165 shorter events, 38.0 us)
Async XLA Ops:
  8.0 33.2 %copy-start.15 = (f32[96,27,1]{0,1,2:T(8,128)S(1)}, f32[96,27,1]{0,1,2:T(8,128)}, u32[]{:S(2)}) copy-start(f32[96,27,1]{0,1,2:T(8,128)} %constant.193) | copy-start | bytes 31108
  8.0 33.7 %copy-start.21 = (f32[96,27,1]{0,1,2:T(8,128)S(1)}, f32[96,27,1]{0,1,2:T(8,128)}, u32[]{:S(2)}) copy-start(f32[96,27,1]{0,1,2:T(8,128)} %constant.195) | copy-start | bytes 31108
  19.5 73.9 %collective-permute-start = (f32[3,729]{1,0:T(4,128)S(1)}, f32[3,729]{1,0:T(4,128)S(1)}, u32[]{:S(2)}, u32[]{:S(2)}) collective-permute-start(f32[3,729]{1,0:T(4,128)S(1)} %slice.223), channel_id=1, source_target_pairs={{0,1},{1,2},{2,3},{4,5},{5,6},{6,7},{8,9},{9,10},{10,11},{12,13},{... | collective-permute-start | bytes 26252
  25.3 121.1 %all-to-all-start = ((f32[64,1,4,1,729]{4,2,3,1,0:T(4,128)}), f32[64,1,4,1,729]{4,2,3,1,0:T(4,128)}, u32[]{:S(2)}, u32[]{:S(2)}) async-start(f32[64,1,4,1,729]{4,2,3,1,0:T(4,128)} %broadcast_in_dim.45), calls=%async_computation | async-start | bytes 1572864 | tf_op jit(solution)/shard_map/all_to_all | solution.py:50
  40.5 105.5 %all-reduce.5.cloned.1.call-start = ((), (), s32[]{:S(2)}) async-start(), calls=%async_computation.1 | async-start | bytes 196608 | tf_op jit(solution)/shard_map/psum | solution.py:206
  58.1 5.5 %copy-start.17 = (f32[96,27]{0,1:T(8,128)S(1)}, f32[96,27]{0,1:T(8,128)}, u32[]{:S(2)}) copy-start(f32[96,27]{0,1:T(8,128)} %constant.177.clone) | copy-start | bytes 31108
  61.8 6.5 %copy-start.8 = (f32[27,9216]{1,0:T(8,128)S(1)}, f32[27,9216]{1,0:T(8,128)}, u32[]{:S(2)}) copy-start(f32[27,9216]{1,0:T(8,128)} %reshape.439) | copy-start | bytes 2985988
  68.3 6.0 %copy-start.4 = (f32[96,9216]{1,0:T(8,128)}, f32[96,9216]{1,0:T(8,128)S(1)}, u32[]{:S(2)}) copy-start(f32[96,9216]{1,0:T(8,128)S(1)} %fusion.68) | copy-start | bytes 10616836
  71.3 4.8 %copy-start = (f32[1,96,9216]{2,1,0:T(8,128)S(1)}, f32[1,96,9216]{2,1,0:T(8,128)}, u32[]{:S(2)}) copy-start(f32[1,96,9216]{2,1,0:T(8,128)} %param.21) | copy-start | bytes 10616836
  71.3 4.8 %copy-start.18 = (f32[96,27]{0,1:T(8,128)S(1)}, f32[96,27]{0,1:T(8,128)}, u32[]{:S(2)}) copy-start(f32[96,27]{0,1:T(8,128)} %constant.179.clone) | copy-start | bytes 31108
  76.2 5.0 %copy-start.14 = (f32[96,27,1]{0,1,2:T(8,128)S(1)}, f32[96,27,1]{0,1,2:T(8,128)}, u32[]{:S(2)}) copy-start(f32[96,27,1]{0,1,2:T(8,128)} %constant.194) | copy-start | bytes 31108
  80.6 5.0 %copy-start.30 = (f32[2]{0:T(128)S(1)}, f32[2]{0:T(128)}, u32[]{:S(2)}) copy-start(f32[2]{0:T(128)} %constant.181.clone) | copy-start | bytes 28
  81.2 10.9 %copy-start.31 = (u32[256]{0:T(256)S(1)}, u32[256]{0:T(256)}, u32[]{:S(2)}) copy-start(u32[256]{0:T(256)} %constant.191) | copy-start | bytes 3076
  83.6 80.6 %all-gather.3.cloned.1.call-start = ((), (), s32[]{:S(2)}) async-start(), calls=%async_computation.2 | async-start | bytes 1597440 | tf_op jit(solution)/shard_map/all_gather | solution.py:243
  108.2 4.4 %copy-start.19 = (f32[96,27]{0,1:T(8,128)S(1)}, f32[96,27]{0,1:T(8,128)}, u32[]{:S(2)}) copy-start(f32[96,27]{0,1:T(8,128)} %constant.179.clone) | copy-start | bytes 31108
  112.7 7.8 %copy-start.2 = (f32[1,96,9216]{2,1,0:T(8,128)S(1)}, f32[1,96,9216]{2,1,0:T(8,128)}, u32[]{:S(2)}) copy-start(f32[1,96,9216]{2,1,0:T(8,128)} %param.20) | copy-start | bytes 10616836
  112.7 7.8 %copy-start.6 = (f32[96,9216]{1,0:T(8,128)S(1)}, f32[96,9216]{1,0:T(8,128)}, u32[]{:S(2)}) copy-start(f32[96,9216]{1,0:T(8,128)} %copy-done.5) | copy-start | bytes 10616836
  112.7 7.8 %copy-start.22 = (f32[96,27]{0,1:T(8,128)S(1)}, f32[96,27]{0,1:T(8,128)}, u32[]{:S(2)}) copy-start(f32[96,27]{0,1:T(8,128)} %constant.180.clone) | copy-start | bytes 31108
  143.8 5.0 %copy-start.13 = (f32[4,2,27,27]{3,1,2,0:T(2,128)S(1)}, f32[4,2,27,27]{3,1,2,0:T(2,128)}, u32[]{:S(2)}) copy-start(f32[4,2,27,27]{3,1,2,0:T(2,128)} %copy-done.12) | copy-start | bytes 69988
  143.8 5.0 %copy-start.27 = (f32[4,2]{1,0:T(4,128)S(1)}, f32[4,2]{1,0:T(4,128)}, u32[]{:S(2)}) copy-start(f32[4,2]{1,0:T(4,128)} %reshape.453) | copy-start | bytes 100
  143.8 5.0 %copy-start.29 = (pred[4,2]{1,0:T(4,128)(4,1)S(1)}, pred[4,2]{1,0:T(4,128)(4,1)}, u32[]{:S(2)}) copy-start(pred[4,2]{1,0:T(4,128)(4,1)} %compare_and_fusion.1) | copy-start | bytes 28
  144.3 4.8 %copy-start.11 = (f32[4,2,27,27]{3,1,2,0:T(2,128)S(1)}, f32[4,2,27,27]{3,1,2,0:T(2,128)}, u32[]{:S(2)}) copy-start(f32[4,2,27,27]{3,1,2,0:T(2,128)} %copy-done.10) | copy-start | bytes 69988
  144.3 19.9 %copy-start.26 = (s32[512]{0:T(512)S(1)}, s32[512]{0:T(512)}, u32[]{:S(2)}) copy-start(s32[512]{0:T(512)} %eq.41) | copy-start | bytes 6148
  144.3 19.9 %copy-start.28 = (pred[512]{0:T(512)(128)(4,1)S(1)}, pred[512]{0:T(512)(128)(4,1)}, u32[]{:S(2)}) copy-start(pred[512]{0:T(512)(128)(4,1)} %and.41) | copy-start | bytes 1540
  (12 other events, 35.0 us)
Sparse Core Ops, SparseCore 0:
  83.8 43.7 all-reduce.4
Sparse Core Ops, SparseCore 1:
  87.4 76.8 all-gather.2
where the time goes:
time: 179 us; the launch traced here: 176 us
  matrix products  60.8 us (34%)
  local copies, waits for them, and re-layouts  41.2 us (23%)
  blocking collectives  19.6 us (11%)
  starting transfers between devices  18.2 us (10%)
  between operations  17.3 us (10%)
  waiting for transfers between devices  14.1 us (8%)
  other arithmetic  4.58 us (3%)
    all_to_all x1, starting transfers between devices, from_everyone(): lax.all_to_all(jnp.broadcast_to(value[None], (peers, *value.shape)), axis...  15.1 us
    all_gather x1, waiting for transfers between devices, per_device(): all_blocks = lax.all_gather(correction, 'patch', axis=0, tiled=True)  14 us
    unnamed x1, blocking collectives  10.5 us
    all_gather x1, blocking collectives, spread(): lax.all_gather(own, axis, axis=0, tiled=True)[:len(lines)]  9.12 us
    dot_general x1, matrix products, backward_sum(): jnp.dot(value_weighted.T, fluxes[2], precision=highest)  8.23 us
    dot_general x1, matrix products, backward_sum(): jnp.dot(value_weighted.T, fluxes[1], precision=highest)  7.78 us
    dot_general x1, matrix products, gradients(): jnp.dot(value_table, mid_second, precision=highest, preferred_element_typ...  4.66 us
    dot_general x1, matrix products, backward(): jnp.dot(outer_matrix.T, values, precision=highest, preferred_element_type...  4.4 us
  transfers between devices with their start and end apart: 4, of which 1 were waited for; matrix products, arithmetic and copies ran while one was open for 57% of the time, Pallas kernels for 0%

commit v1 on v0

--- a/solution.py
+++ b/solution.py
@@ -240,7 +240,9 @@
     correction = (correction * signs[None, :, None, None, None]).reshape(
         item_count, vectors, size_n * size_n
     )
-    all_blocks = lax.all_gather(correction, "patch", axis=0, tiled=True)
+    all_blocks = jnp.concatenate(
+        lax.all_to_all(jnp.stack([correction] * lax.axis_size("patch")), "patch", 0, 0), axis=0
+    )
     face_match = (
         (is_live & (item_patch == device)).reshape(-1)[None, :]
         & (item_face.reshape(-1)[None, :] == face_grid[:, None])

time: 179 us -> 188 us (1.050)
  starting transfers between devices: 18.2 us -> 31.3 us
  waiting for transfers between devices: 14.1 us -> 5.97 us
  matrix products: 60.8 us -> 64.4 us
    all_gather x1 -> x0, waiting for transfers between devices: 14 us -> none  [per_device(): all_blocks = lax.all_gather(correction, 'patch', axis=0, tiled=True)]
    all_to_all x0 -> x1, starting transfers between devices: none -> 13.2 us  [per_device(): lax.all_to_all(jnp.stack([correction] * lax.axis_size('patch')), 'patch',...]
    all_to_all x0 -> x1, waiting for transfers between devices: none -> 5.94 us  [per_device(): lax.all_to_all(jnp.stack([correction] * lax.axis_size('patch')), 'patch',...]
    dot_general x1, matrix products: 4.1 us -> 8.25 us  [backward_sum(): jnp.dot(slope_weighted.T, fluxes[0], precision=highest)]
    another operation x5 -> x7, local copies, waits for them, and re-layouts: 0.5 us -> 3.25 us  [the longest x2 2.75 us: per_device(): jnp.stack([correction] * lax.axis_size('patch'))]
where the time goes in v1:
time: 188 us; the launch traced here: 185 us
  matrix products  64.4 us (34%)
  local copies, waits for them, and re-layouts  42.5 us (23%)
  starting transfers between devices  31.3 us (17%)
  blocking collectives  20.1 us (11%)
  between operations  15.7 us (8%)
  waiting for transfers between devices  5.97 us (3%)
  other arithmetic  4.6 us (2%)
    all_to_all x1, starting transfers between devices, from_everyone(): lax.all_to_all(jnp.broadcast_to(value[None], (peers, *value.shape)), axis...  15.1 us
    all_to_all x1, starting transfers between devices, per_device(): lax.all_to_all(jnp.stack([correction] * lax.axis_size('patch')), 'patch',...  13.2 us
    unnamed x1, blocking collectives  10.5 us
    all_gather x1, blocking collectives, spread(): lax.all_gather(own, axis, axis=0, tiled=True)[:len(lines)]  9.56 us
    dot_general x1, matrix products, backward_sum(): jnp.dot(slope_weighted.T, fluxes[0], precision=highest)  8.25 us
    dot_general x1, matrix products, backward_sum(): jnp.dot(value_weighted.T, fluxes[2], precision=highest)  8.16 us
    dot_general x1, matrix products, backward_sum(): jnp.dot(value_weighted.T, fluxes[1], precision=highest)  7.22 us
    all_to_all x1, waiting for transfers between devices, per_device(): lax.all_to_all(jnp.stack([correction] * lax.axis_size('patch')), 'patch',...  5.94 us
  transfers between devices with their start and end apart: 4, of which 1 were waited for; matrix products, arithmetic and copies ran while one was open for 57% of the time, Pallas kernels for 0%

profile of v1, /device:TPU:1, one launch (start us, length us, event | category | flops | bytes accessed | tf_op | source)
XLA Modules:
  0.0 184.5 jit_solution(6810072813569362978)
XLA Ops:
  8.1 10.5 %fusion = f32[8,729]{1,0:T(8,128)S(1)} fusion(f32[28,729]{1,0:T(8,128)S(1)} %concatenate.12), kind=kCustom, calls=%all-reduce-scatter | all-reduce-scatter fusion | flops 23329 | bytes 106000
  18.7 2.8 %collective-permute-start = (f32[3,729]{1,0:T(4,128)S(1)}, f32[3,729]{1,0:T(4,128)S(1)}, u32[]{:S(2)}, u32[]{:S(2)}) collective-permute-start(f32[3,729]{1,0:T(4,128)S(1)} %slice.223), channel_id=1, source_target_pairs={{0,1},{1,2},{2,3},{4,5},{5,6},{6,7},{8,9},{9,10},{10,11},{12,13},{... | collective-permute-start | bytes 26252
  24.5 15.1 %all-to-all-start.1 = ((f32[64,1,4,1,729]{4,2,3,1,0:T(4,128)}), f32[64,1,4,1,729]{4,2,3,1,0:T(4,128)}, u32[]{:S(2)}, u32[]{:S(2)}) async-start(f32[64,1,4,1,729]{4,2,3,1,0:T(4,128)} %broadcast_in_dim.45), calls=%async_computation.1 | async-start | bytes 1572864 | tf_op jit(solution)/shard_map/all_to_all | solution.py:50
  41.4 2.2 %convolution_bitcast_fusion.1 = f32[27,96,96]{1,2,0:T(8,128)S(1)} fusion(f32[27,27,96]{2,1,0:T(8,128)S(1)} %convolution_bitcast_fusion.7, f32[96,27,1]{0,1,2:T(8,128)S(1)} %copy-done.19), kind=kOutput, calls=%fused_computation.38 | convolution fusion | flops 80621568 | bytes 1285632 | tf_op jit(solution)/shard_map/while/body/eval_jaxpr/bj,ijc->ibc/dot_general | solution.py:137
  43.6 2.2 %convolution_bitcast_fusion.3 = f32[27,96,96]{1,2,0:T(8,128)S(1)} fusion(f32[27,27,96]{2,1,0:T(8,128)S(1)} %convolution_bitcast_fusion.7, f32[96,27,1]{0,1,2:T(8,128)S(1)} %copy-done.13), kind=kOutput, calls=%fused_computation.40 | convolution fusion | flops 80621568 | bytes 1285632 | tf_op jit(solution)/shard_map/while/body/eval_jaxpr/bj,ijc->ibc/dot_general | solution.py:134
  46.5 3.3 %convolution_bitcast_fusion = f32[27,96,96]{1,2,0:T(8,128)} fusion(f32[27,27,96]{2,1,0:T(8,128)S(1)} %convolution_bitcast_fusion.6, f32[96,27,1]{0,1,2:T(8,128)S(1)} %copy-done.13), kind=kOutput, calls=%fused_computation.37 | convolution fusion | flops 80621568 | bytes 1285632 | tf_op jit(solution)/shard_map/while/body/eval_jaxpr/bj,ijc->ibc/dot_general | solution.py:140
  49.8 2.8 %copy.46 = f32[27,96,96]{2,1,0:T(8,128)} copy(f32[27,96,96]{1,2,0:T(8,128)} %convolution_bitcast_fusion) | data formatting | bytes 1990656 | tf_op jit(solution)/shard_map/while/body/eval_jaxpr/bj,ijc->ibc/transpose | solution.py:140
  52.6 3.2 %reshape.442 = f32[27,9216]{1,0:T(8,128)} reshape(f32[27,96,96]{2,1,0:T(8,128)} %copy.46) | data formatting | bytes 1990656 | tf_op jit(solution)/shard_map/while/body/eval_jaxpr/reshape | solution.py:140
  57.3 3.2 %reshape.440 = f32[27,9216]{1,0:T(8,128)} reshape(f32[27,96,96]{2,1,0:T(8,128)} %copy.45) | data formatting | bytes 1990656 | tf_op jit(solution)/shard_map/while/body/eval_jaxpr/reshape | solution.py:137
  62.8 4.7 %fusion.68 = f32[96,9216]{1,0:T(8,128)S(1)} fusion(f32[96,27]{0,1:T(8,128)S(1)} %copy-done.15, f32[27,9216]{1,0:T(8,128)} %reshape.440), kind=kOutput, calls=%fused_computation.118 | convolution fusion | flops 286654464 | bytes 4544640 | tf_op jit(solution)/shard_map/while/body/eval_jaxpr/dot_general | solution.py:145
  67.5 3.0 %fusion.70 = f32[96,9216]{1,0:T(8,128)S(1)} fusion(f32[96,27]{0,1:T(8,128)S(1)} %copy-done.15, f32[27,9216]{1,0:T(8,128)S(1)} %copy-done.6), kind=kOutput, calls=%fused_computation.120 | convolution fusion | flops 286654464 | bytes 4544640 | tf_op jit(solution)/shard_map/while/body/eval_jaxpr/dot_general | solution.py:146
  70.5 3.0 %fusion.64 = f32[96,9216]{1,0:T(8,128)S(1)} fusion(f32[96,27]{0,1:T(8,128)S(1)} %copy-done.20, f32[27,9216]{1,0:T(8,128)S(1)} %copy-done.7), kind=kOutput, calls=%fused_computation.114 | convolution fusion | flops 286654464 | bytes 4544640 | tf_op jit(solution)/shard_map/while/body/eval_jaxpr/dot_general | solution.py:144
  75.3 4.4 %fusion.13 = f32[27,9216]{1,0:T(8,128)S(1)} fusion(f32[96,27]{0,1:T(8,128)S(1)} %copy-done.16, f32[1,96,9216]{2,1,0:T(8,128)S(1)} %copy-done, f32[96,9216]{1,0:T(8,128)S(1)} %fusion.70, f32[96,9216]{1,0:T(8,128)S(1)} %fusion.68, f32[96,9216]{1,0:T(8,128)S(1)} %fusion.64, f32[]{:T(128)} %bitcast.17, f32[]{:T(128)} %bitcast.12, f32[]{:T(128)} %bitcast.4), kind=kOutput, calls=%fused_computation.14 | convolution fusion | flops 291962880 | bytes 15161484 | tf_op jit(solution)/shard_map/while/body/eval_jaxpr/dot_general | solution.py:120
  92.2 9.6 %all-gather = f32[4,7,729]{2,1,0:T(8,128)S(1)} all-gather(f32[1,7,729]{2,1,0:T(8,128)S(1)} %dynamic-slice_bitcast_fusion), channel_id=1, replica_groups=mesh['patch'=64,'sub'=4] {'sub'}, dimensions={0}, use_global_device_ids=true | all-gather | bytes 102060 | tf_op jit(solution)/shard_map/all_gather | solution.py:39
  102.7 2.2 %convolution_bitcast_fusion.2 = f32[27,96,96]{1,2,0:T(8,128)S(1)} fusion(f32[27,27,96]{2,1,0:T(8,128)S(1)} %fusion.65, f32[96,27,1]{0,1,2:T(8,128)S(1)} %copy-done.13), kind=kOutput, calls=%fused_computation.39 | convolution fusion | flops 80621568 | bytes 1285632 | tf_op jit(solution)/shard_map/while/body/eval_jaxpr/bj,ijc->ibc/dot_general | solution.py:108
  107.3 4.4 %fusion.66 = f32[96,9216]{1,0:T(8,128)S(1)} fusion(f32[96,27]{0,1:T(8,128)} %constant.177.clone, f32[27,9216]{1,0:T(8,128)} %reshape.438), kind=kOutput, calls=%fused_computation.116 | convolution fusion | flops 286654464 | bytes 4544640 | tf_op jit(solution)/shard_map/while/body/eval_jaxpr/dot_general | solution.py:109
  111.7 7.2 %fusion.7 = f32[27,9216]{1,0:T(8,128)} fusion(f32[96,27]{0,1:T(8,128)S(1)} %copy-done.17, f32[96,9216]{1,0:T(8,128)S(1)} %fusion.66, f32[1,96,9216]{2,1,0:T(8,128)S(1)} %copy-done.1, f32[96,9216]{1,0:T(8,128)} %copy-done.4, f32[1,96,9216]{2,1,0:T(8,128)} %param.20, f32[]{:T(128)} %bitcast.12, f32[]{:T(128)S(6)} %select_n.60), kind=kOutput, calls=%fused_computation.10 | convolution fusion | flops 291078144 | bytes 15161480 | tf_op jit(solution)/shard_map/while/body/eval_jaxpr/dot_general | solution.py:156
  120.9 13.2 %all-to-all-start = ((f32[64,8,1,729]{3,1,2,0:T(8,128)}), f32[64,8,1,729]{3,1,2,0:T(8,128)}, u32[]{:S(2)}, u32[]{:S(2)}) async-start(f32[64,8,1,729]{3,1,2,0:T(8,128)} %stack.14), calls=%async_computation | async-start | bytes 3145728 | tf_op jit(solution)/shard_map/all_to_all | solution.py:244
  134.2 8.3 %fusion.3 = f32[27,9216]{1,0:T(8,128)} fusion(f32[96,27]{0,1:T(8,128)} %constant.180.clone, f32[96,9216]{1,0:T(8,128)S(1)} %fusion.66, f32[1,96,9216]{2,1,0:T(8,128)} %param.21, f32[96,9216]{1,0:T(8,128)} %copy-done.3, f32[1,96,9216]{2,1,0:T(8,128)} %param.20, f32[]{:T(128)} %bitcast.4, f32[]{:T(128)S(6)} %select_n.60), kind=kOutput, calls=%fused_computation.7 | convolution fusion | flops 291078144 | bytes 15161480 | tf_op jit(solution)/shard_map/while/body/eval_jaxpr/dot_general | solution.py:153
  142.4 2.9 %reshape.439 = f32[27,96,96]{2,1,0:T(8,128)} reshape(f32[27,9216]{1,0:T(8,128)} %fusion.3) | data formatting | bytes 1990656 | tf_op jit(solution)/shard_map/while/body/eval_jaxpr/reshape | solution.py:153
  145.3 2.9 %reshape.441 = f32[27,96,96]{2,1,0:T(8,128)} reshape(f32[27,9216]{1,0:T(8,128)} %fusion.7) | data formatting | bytes 1990656 | tf_op jit(solution)/shard_map/while/body/eval_jaxpr/reshape | solution.py:156
  148.2 8.2 %fusion.11 = f32[27,9216]{1,0:T(8,128)} fusion(f32[96,27]{0,1:T(8,128)} %constant.179.clone, f32[96,9216]{1,0:T(8,128)S(1)} %fusion.66, f32[1,96,9216]{2,1,0:T(8,128)} %param.21, f32[96,9216]{1,0:T(8,128)} %copy-done.2, f32[1,96,9216]{2,1,0:T(8,128)} %param.20, f32[]{:T(128)} %bitcast.17, f32[]{:T(128)S(6)} %select_n.60), kind=kOutput, calls=%fused_computation.13 | convolution fusion | flops 291078144 | bytes 15161480 | tf_op jit(solution)/shard_map/while/body/eval_jaxpr/dot_general | solution.py:159
  158.2 2.2 %fusion.67 = f32[27,96,27]{1,2,0:T(8,128)S(1)} fusion(f32[27,96,96]{2,1,0:T(8,128)} %reshape.439, f32[96,27,1]{0,1,2:T(8,128)S(1)} %copy-done.12), kind=kOutput, calls=%fused_computation.117 | convolution fusion | flops 80621568 | bytes 1285632 | tf_op jit(solution)/shard_map/while/body/eval_jaxpr/bj,ibc->ijc/dot_general | solution.py:162
  167.7 5.9 %all-to-all-done = f32[64,8,1,729]{3,1,2,0:T(8,128)} async-done(((f32[64,8,1,729]{3,1,2,0:T(8,128)}), f32[64,8,1,729]{3,1,2,0:T(8,128)}, u32[]{:S(2)}, u32[]{:S(2)}) %all-to-all-start) | async-done | bytes 1493024 | tf_op jit(solution)/shard_map/all_to_all | solution.py:244
  (159 shorter events, 41.5 us)
Async XLA Ops:
  7.2 33.2 %copy-start.13 = (f32[96,27,1]{0,1,2:T(8,128)S(1)}, f32[96,27,1]{0,1,2:T(8,128)}, u32[]{:S(2)}) copy-start(f32[96,27,1]{0,1,2:T(8,128)} %constant.193) | copy-start | bytes 31108
  7.2 33.7 %copy-start.19 = (f32[96,27,1]{0,1,2:T(8,128)S(1)}, f32[96,27,1]{0,1,2:T(8,128)}, u32[]{:S(2)}) copy-start(f32[96,27,1]{0,1,2:T(8,128)} %constant.195) | copy-start | bytes 31108
  18.7 73.4 %collective-permute-start = (f32[3,729]{1,0:T(4,128)S(1)}, f32[3,729]{1,0:T(4,128)S(1)}, u32[]{:S(2)}, u32[]{:S(2)}) collective-permute-start(f32[3,729]{1,0:T(4,128)S(1)} %slice.223), channel_id=1, source_target_pairs={{0,1},{1,2},{2,3},{4,5},{5,6},{6,7},{8,9},{9,10},{10,11},{12,13},{... | collective-permute-start | bytes 26252
  24.5 94.4 %all-to-all-start.1 = ((f32[64,1,4,1,729]{4,2,3,1,0:T(4,128)}), f32[64,1,4,1,729]{4,2,3,1,0:T(4,128)}, u32[]{:S(2)}, u32[]{:S(2)}) async-start(f32[64,1,4,1,729]{4,2,3,1,0:T(4,128)} %broadcast_in_dim.45), calls=%async_computation.1 | async-start | bytes 1572864 | tf_op jit(solution)/shard_map/all_to_all | solution.py:50
  39.7 123.9 %all-reduce.5.cloned.1.call-start = ((), (), s32[]{:S(2)}) async-start(), calls=%async_computation.2 | async-start | bytes 196608 | tf_op jit(solution)/shard_map/psum | solution.py:206
  57.3 5.5 %copy-start.15 = (f32[96,27]{0,1:T(8,128)S(1)}, f32[96,27]{0,1:T(8,128)}, u32[]{:S(2)}) copy-start(f32[96,27]{0,1:T(8,128)} %constant.177.clone) | copy-start | bytes 31108
  60.9 6.5 %copy-start.6 = (f32[27,9216]{1,0:T(8,128)S(1)}, f32[27,9216]{1,0:T(8,128)}, u32[]{:S(2)}) copy-start(f32[27,9216]{1,0:T(8,128)} %reshape.442) | copy-start | bytes 2985988
  67.5 6.0 %copy-start.4 = (f32[96,9216]{1,0:T(8,128)}, f32[96,9216]{1,0:T(8,128)S(1)}, u32[]{:S(2)}) copy-start(f32[96,9216]{1,0:T(8,128)S(1)} %fusion.68) | copy-start | bytes 10616836
  70.5 4.8 %copy-start = (f32[1,96,9216]{2,1,0:T(8,128)S(1)}, f32[1,96,9216]{2,1,0:T(8,128)}, u32[]{:S(2)}) copy-start(f32[1,96,9216]{2,1,0:T(8,128)} %param.21) | copy-start | bytes 10616836
  70.5 4.8 %copy-start.16 = (f32[96,27]{0,1:T(8,128)S(1)}, f32[96,27]{0,1:T(8,128)}, u32[]{:S(2)}) copy-start(f32[96,27]{0,1:T(8,128)} %constant.179.clone) | copy-start | bytes 31108
  75.3 5.0 %copy-start.12 = (f32[96,27,1]{0,1,2:T(8,128)S(1)}, f32[96,27,1]{0,1,2:T(8,128)}, u32[]{:S(2)}) copy-start(f32[96,27,1]{0,1,2:T(8,128)} %constant.194) | copy-start | bytes 31108
  79.8 5.8 %copy-start.14 = (f32[4,2,2,27,27]{4,2,3,1,0:T(2,128)S(1)}, f32[4,2,2,27,27]{4,2,3,1,0:T(2,128)}, u32[]{:S(2)}) copy-start(f32[4,2,2,27,27]{4,2,3,1,0:T(2,128)} %param.23) | copy-start | bytes 139972
  79.8 6.9 %copy-start.27 = (f32[2]{0:T(128)S(1)}, f32[2]{0:T(128)}, u32[]{:S(2)}) copy-start(f32[2]{0:T(128)} %constant.181.clone) | copy-start | bytes 28
  80.3 10.6 %copy-start.28 = (u32[256]{0:T(256)S(1)}, u32[256]{0:T(256)}, u32[]{:S(2)}) copy-start(u32[256]{0:T(256)} %constant.191) | copy-start | bytes 3076
  107.3 4.4 %copy-start.1 = (f32[1,96,9216]{2,1,0:T(8,128)S(1)}, f32[1,96,9216]{2,1,0:T(8,128)}, u32[]{:S(2)}) copy-start(f32[1,96,9216]{2,1,0:T(8,128)} %param.21) | copy-start | bytes 10616836
  107.3 4.4 %copy-start.17 = (f32[96,27]{0,1:T(8,128)S(1)}, f32[96,27]{0,1:T(8,128)}, u32[]{:S(2)}) copy-start(f32[96,27]{0,1:T(8,128)} %constant.179.clone) | copy-start | bytes 31108
  120.9 52.7 %all-to-all-start = ((f32[64,8,1,729]{3,1,2,0:T(8,128)}), f32[64,8,1,729]{3,1,2,0:T(8,128)}, u32[]{:S(2)}, u32[]{:S(2)}) async-start(f32[64,8,1,729]{3,1,2,0:T(8,128)} %stack.14), calls=%async_computation | async-start | bytes 3145728 | tf_op jit(solution)/shard_map/all_to_all | solution.py:244
  156.3 4.1 %copy-start.18 = (f32[96,27,1]{0,1,2:T(8,128)S(1)}, f32[96,27,1]{0,1,2:T(8,128)}, u32[]{:S(2)}) copy-start(f32[96,27,1]{0,1,2:T(8,128)} %constant.196) | copy-start | bytes 31108
  161.3 4.9 %copy-start.11 = (f32[4,2,27,27]{3,1,2,0:T(2,128)S(1)}, f32[4,2,27,27]{3,1,2,0:T(2,128)}, u32[]{:S(2)}) copy-start(f32[4,2,27,27]{3,1,2,0:T(2,128)} %copy-done.10) | copy-start | bytes 69988
  161.3 4.9 %copy-start.24 = (f32[4,2]{1,0:T(4,128)S(1)}, f32[4,2]{1,0:T(4,128)}, u32[]{:S(2)}) copy-start(f32[4,2]{1,0:T(4,128)} %reshape.455) | copy-start | bytes 100
  161.4 4.9 %copy-start.26 = (pred[4,2]{1,0:T(4,128)(4,1)S(1)}, pred[4,2]{1,0:T(4,128)(4,1)}, u32[]{:S(2)}) copy-start(pred[4,2]{1,0:T(4,128)(4,1)} %compare_and_fusion.1) | copy-start | bytes 28
  161.9 4.8 %copy-start.9 = (f32[4,2,27,27]{3,1,2,0:T(2,128)S(1)}, f32[4,2,27,27]{3,1,2,0:T(2,128)}, u32[]{:S(2)}) copy-start(f32[4,2,27,27]{3,1,2,0:T(2,128)} %copy-done.8) | copy-start | bytes 69988
  161.9 11.8 %copy-start.23 = (s32[512]{0:T(512)S(1)}, s32[512]{0:T(512)}, u32[]{:S(2)}) copy-start(s32[512]{0:T(512)} %eq.41) | copy-start | bytes 6148
  161.9 11.8 %copy-start.25 = (pred[512]{0:T(512)(128)(4,1)S(1)}, pred[512]{0:T(512)(128)(4,1)}, u32[]{:S(2)}) copy-start(pred[512]{0:T(512)(128)(4,1)} %and.41) | copy-start | bytes 1540
  (9 other events, 22.8 us)
Sparse Core Ops, SparseCore 0:
  82.9 43.8 all-reduce.4
